TPU v7x, 256 devices: a 2x2x32 block of a 4x8x32 slice. The times are simulated.
256 devices in a mesh: groups: 4 (over x, y), blk: 64 (over z, core).
Axes of the slice: x: 2, y: 2, z: 32, core: 2. Of those that a mesh axis runs over, the one named last changes fastest.
The devices are a block of a 4x8x32 slice.
Arguments:
- queries: bfloat16 [8192, 8192], P('groups', 'blk'), parts along dimension 0, may hold values from -41 to 41
- prefix_kv: bfloat16 [256, 64, 8, 256], P(('groups', 'blk')), parts along dimension 0, may hold values from -6 to 6
- page_counts: int32 [16], P('groups'), parts along dimension 0, may hold values from 1 to 32, 64 in all
- request_prefix: int32 [8192, 1], P(('groups', 'blk')), parts along dimension 0, may hold values from 0 to 3
- suffix_kv: bfloat16 [8192, 64, 8, 256], P(('groups', 'blk')), parts along dimension 0, may hold values from -6 to 6
- suffix_len: int32 [8192], P(('groups', 'blk')), parts along dimension 0, may hold values from 2 to 64, as said below
Outputs:
- attended: bfloat16 [8192, 8192], P('groups', 'blk'), parts along dimension 0
There are 4 independent parts, one for each index of `groups`. A program takes and returns all parts, laid end to end along the dimension named above; each array names one. Nothing has to cross between parts.
Inputs may be any that keep to these rules, and one draw needn't show every extreme that they name: `page_counts`: the counts sum to 64; the largest is exactly half of 64. `request_prefix`: every prefix is named by some request. `suffix_len`: the requests of one device (aligned blocks of 32) include one with 64 live positions.
All inputs are finite; a program needn't handle non-finite values.
Results may differ from a plain program's by a relative error of at most 0.013.
Values may be sent and summed in bfloat16 or wider, within the bound.
No kernel may reach another device: no remote copies, remote signals or barrier semaphores. Data moves between devices by JAX's collectives and lax.ppermute only.
A program may use at most 64 MiB of HBM per device.

v0:
```python
import functools

import jax
import jax.numpy as jnp
from jax import lax
from jax.experimental import pallas as pl
from jax.experimental.pallas import tpu as pltpu
from jax.sharding import Mesh
from jax.sharding import PartitionSpec as P

SEGS = 8
CORES = 2
BLK = ("seg", "chip", "core")
GROUPS_BLK = ("groups", "seg", "chip", "core")


LOG2E = 1.4426950408889634
LN2 = 0.6931471805599453
NEG = -1e30

REQ_STEP = 8
TOK_BLOCK = 512
ROW_BLOCK = 512

NT = (((1,), (1,)), ((), ()))


def f32(x):
    return x.astype(jnp.float32)


def bf16(x):
    return x.astype(jnp.bfloat16)


def suffix_kernel(
    len_ref, got_ref, owner_ref, cache_ref, out_ref, kv_ref, sems, q_scr, o_scr, s_scr, w_scr, t_scr, bias_scr, *, req_dev, heads, kv_heads
):
    def fetch(step):
        at = pl.ds(step * REQ_STEP, REQ_STEP)
        return pltpu.make_async_copy(cache_ref.at[at], kv_ref.at[at], sems.at[step])

    for step in range(req_dev // REQ_STEP):
        fetch(step).start()
    hd = q_scr.shape[1]
    cols = kv_ref.shape[1]
    stride = out_ref.shape[0] // heads
    scale = hd**-0.5 * LOG2E
    lane = lax.broadcasted_iota(jnp.int32, (heads, hd), 1)

    for h in range(heads):
        q_scr[pl.ds(h, req_dev, stride=heads), :] = f32(got_ref[h, 0:req_dev, :])
    row = lax.broadcasted_iota(jnp.int32, (heads, cols), 0)
    col = lax.broadcasted_iota(jnp.int32, (heads, cols), 1)
    same = (col % kv_heads) == (row // (heads // kv_heads))
    bias_scr[...] = jnp.where(same, 0.0, NEG)
    col = lax.broadcasted_iota(jnp.int32, (1, cols), 1)

    steps = req_dev // REQ_STEP
    lse = jnp.zeros((heads, hd), jnp.float32)

    def scores(t):
        for i in range(REQ_STEP):
            r = t * REQ_STEP + i
            q = bf16(q_scr[r * heads : (r + 1) * heads, :])
            s_scr[t % 2, i] = lax.dot_general(q, kv_ref[r, :, 0:hd], NT, preferred_element_type=jnp.float32)

    def weights(t, lse):
        for i in range(REQ_STEP):
            r = t * REQ_STEP + i
            past = jnp.where(col < len_ref[r] * kv_heads, 0.0, NEG)
            s = s_scr[t % 2, i] * scale + (bias_scr[...] + past)
            top = jnp.max(s, axis=1, keepdims=True)
            w = jnp.exp2(s - top)
            total = jnp.sum(w, axis=1, keepdims=True)
            w_scr[t % 2, i] = bf16(w)
            t_scr[t % 2, i] = jnp.broadcast_to(total, (heads, hd))
            lse = jnp.where((lane % req_dev) == r, top * LN2 + jnp.log(total), lse)
        return lse

    def mix(t):
        for i in range(REQ_STEP):
            r = t * REQ_STEP + i
            o = jnp.dot(w_scr[t % 2, i], kv_ref[r, :, hd:], preferred_element_type=jnp.float32)
            o_scr[pl.ds(r, heads, stride=stride), :] = o / t_scr[t % 2, i]

    for t in range(steps + 2):
        if t < steps:
            fetch(t).wait()
            scores(t)
        if 0 <= t - 1 < steps:
            lse = weights(t - 1, lse)
        if t >= 2:
            mix(t - 2)

    hi = f32(bf16(lse))
    rest = lse - hi
    mid = f32(bf16(rest))
    low = rest - mid
    extra = jnp.where(lane < req_dev, hi, jnp.where(lane < 2 * req_dev, mid, low))
    extra = jnp.where(lane < 3 * req_dev, extra, owner_ref[...])
    o_scr[pl.ds(req_dev, heads, stride=stride), :] = extra
    o_scr[pl.ds(req_dev + 1, heads, stride=stride), :] = jnp.zeros((heads, hd), jnp.float32)
    n = out_ref.shape[0]
    c = n // 17 if n % 17 == 0 else n

    @pl.loop(0, n // c)
    def _(k):
        at = pl.ds(pl.multiple_of(k * c, 16), c)
        out_ref[at, :] = bf16(o_scr[at, :])


def suffix_attention(got, owner_row, cache, suffix_len, kv_heads):
    req_dev, cols, width = cache.shape
    hd = width // 2
    heads = got.shape[0]
    rows = heads * (req_dev + 2)
    kernel = functools.partial(suffix_kernel, req_dev=req_dev, heads=heads, kv_heads=kv_heads)
    vmem = pl.BlockSpec(memory_space=pltpu.VMEM)
    return pl.pallas_call(
        kernel,
        name="suffix",
        out_shape=jax.ShapeDtypeStruct((rows, hd), jnp.bfloat16),
        in_specs=[pl.BlockSpec(memory_space=pltpu.SMEM), vmem, vmem, pl.BlockSpec(memory_space=pltpu.HBM)],
        out_specs=vmem,
        scratch_shapes=[
            pltpu.VMEM(cache.shape, cache.dtype),
            pltpu.SemaphoreType.DMA((req_dev // REQ_STEP,)),
            pltpu.VMEM((req_dev * heads, hd), jnp.float32),
            pltpu.VMEM((rows, hd), jnp.float32),
            pltpu.VMEM((2, REQ_STEP, heads, cols), jnp.float32),
            pltpu.VMEM((2, REQ_STEP, heads, cols), jnp.bfloat16),
            pltpu.VMEM((2, REQ_STEP, heads, hd), jnp.float32),
            pltpu.VMEM((heads, cols), jnp.float32),
        ],
        compiler_params=pltpu.CompilerParams(vmem_limit_bytes=57 << 20),
        cost_estimate=pl.CostEstimate(
            flops=4 * req_dev * heads * cols * hd,
            bytes_accessed=2 * cache.size,
            transcendentals=req_dev * heads * cols,
        ),
    )(suffix_len, got, owner_row, cache)


def prefix_kernel(count_ref, q_ref, *refs, req_dev, n_chunks):
    chunks = refs[:n_chunks]
    o_ref, lse_ref, k_scr, v_scr, top_scr, sum_scr, acc_scr = refs[n_chunks:]
    n_prefix = o_ref.shape[0]
    n_rows, hd = q_ref.shape
    pages, both = chunks[0].shape[:2]
    tok = both // 2
    page = tok * n_chunks
    scale = hd**-0.5 * LOG2E
    tail = k_scr.shape[0] - pages * page

    @pl.loop(0, pages)
    def _(p):
        for c in range(0, n_chunks, 2):
            a, b = f32(chunks[c][p]), f32(chunks[c + 1][p])
            at = pl.ds(pl.multiple_of(p * page + c * tok, 2 * tok), 2 * tok)
            k_scr[at, :] = bf16(jnp.concatenate([a[:tok], b[:tok]], axis=0))
            v_scr[at, :] = bf16(jnp.concatenate([a[tok:], b[tok:]], axis=0))

    k_scr[pl.ds(pages * page, tail), :] = jnp.zeros((tail, hd), jnp.bfloat16)
    v_scr[pl.ds(pages * page, tail), :] = jnp.zeros((tail, hd), jnp.bfloat16)

    col = lax.broadcasted_iota(jnp.int32, (1, TOK_BLOCK), 1)
    lane = lax.broadcasted_iota(jnp.int32, (req_dev, lse_ref.shape[2]), 1)
    for p in range(n_prefix):
        lse_ref[p] = jnp.zeros(lse_ref.shape[1:], jnp.float32)
    first = 0
    for p in range(n_prefix):
        start = first * page
        live = count_ref[p] * page

        @pl.loop(0, n_rows // ROW_BLOCK)
        def _(rb):
            rows = pl.ds(pl.multiple_of(rb * ROW_BLOCK, ROW_BLOCK), ROW_BLOCK)
            top_scr[...] = jnp.full_like(top_scr, NEG)
            sum_scr[...] = jnp.zeros_like(sum_scr)
            acc_scr[...] = jnp.zeros_like(acc_scr)

            @pl.loop(0, (live + TOK_BLOCK - 1) // TOK_BLOCK)
            def _(b):
                at = pl.ds(pl.multiple_of(start + b * TOK_BLOCK, page), TOK_BLOCK)
                s = lax.dot_general(q_ref[rows, :], k_scr[at, :], NT, preferred_element_type=jnp.float32)
                past = jnp.where(col < live - b * TOK_BLOCK, 0.0, NEG)
                s = s * scale + past
                old = top_scr[...]
                new = jnp.maximum(old, jnp.max(s, axis=1, keepdims=True))
                alpha = jnp.exp2(old - new)
                w = jnp.exp2(s - new[:, 0:1])
                part = w[:, 0:hd]
                for k in range(hd, TOK_BLOCK, hd):
                    part = part + w[:, k : k + hd]
                top_scr[...] = new
                sum_scr[...] = sum_scr[...] * alpha + part
                acc_scr[...] = acc_scr[...] * alpha + jnp.dot(
                    bf16(w), v_scr[at, :], preferred_element_type=jnp.float32
                )

            total = jnp.sum(sum_scr[...], axis=1, keepdims=True)
            o_ref[p, rows, :] = bf16(acc_scr[...] / total)
            value = top_scr[...][:, 0:1] * LN2 + jnp.log(total)
            lse = lse_ref[p]
            for k in range(ROW_BLOCK // req_dev):
                piece = value[k * req_dev : (k + 1) * req_dev, :]
                lse = jnp.where(lane == rb * (ROW_BLOCK // req_dev) + k, piece, lse)
            lse_ref[p] = lse

        first = first + count_ref[p]


def prefix_attention(queries, chunks, page_counts, req_dev):
    n_rows, hd = queries.shape
    n_prefix = page_counts.shape[0]
    pages, both, _ = chunks[0].shape
    tokens = pages * (both // 2) * len(chunks)
    vmem = pl.BlockSpec(memory_space=pltpu.VMEM)
    kernel = functools.partial(prefix_kernel, req_dev=req_dev, n_chunks=len(chunks))
    return pl.pallas_call(
        kernel,
        name="prefix",
        out_shape=(
            jax.ShapeDtypeStruct((n_prefix, n_rows, hd), jnp.bfloat16),
            jax.ShapeDtypeStruct((n_prefix, req_dev, hd), jnp.float32),
        ),
        in_specs=[pl.BlockSpec(memory_space=pltpu.SMEM)] + [vmem] * (1 + len(chunks)),
        out_specs=(vmem, vmem),
        scratch_shapes=[
            pltpu.VMEM((tokens + TOK_BLOCK, hd), jnp.bfloat16),
            pltpu.VMEM((tokens + TOK_BLOCK, hd), jnp.bfloat16),
            pltpu.VMEM((ROW_BLOCK, hd), jnp.float32),
            pltpu.VMEM((ROW_BLOCK, hd), jnp.float32),
            pltpu.VMEM((ROW_BLOCK, hd), jnp.float32),
        ],
        compiler_params=pltpu.CompilerParams(vmem_limit_bytes=24 << 20),
        cost_estimate=pl.CostEstimate(
            flops=4 * n_rows * tokens * hd, bytes_accessed=4 * n_rows * hd, transcendentals=n_rows * tokens
        ),
    )(page_counts, queries, *chunks)


def combine_kernel(got_ref, o_ref, lse_ref, out_ref, scr, *, req_dev):
    n, hd = scr.shape
    stride = req_dev + 2
    blocks = n // stride
    n_prefix = o_ref.shape[0]
    c = n // 17 if n % 17 == 0 else n

    @pl.loop(0, n // c)
    def _(k):
        at = pl.ds(pl.multiple_of(k * c, 16), c)
        scr[at, :] = f32(got_ref[at, :])

    extra = scr[pl.ds(req_dev, blocks, stride=stride), :].T
    tall = [extra[k * req_dev : (k + 1) * req_dev, :] for k in range(4)]
    suffix_lse = tall[0] + tall[1] + tall[2]
    owner = tall[3]
    prefix_lse = lse_ref[0][:, 0:blocks]
    for p in range(1, n_prefix):
        prefix_lse = jnp.where(owner == p, lse_ref[p][:, 0:blocks], prefix_lse)
    top = jnp.maximum(suffix_lse, prefix_lse)
    ws = jnp.exp(suffix_lse - top)
    wp = jnp.exp(prefix_lse - top)
    inverse = 1.0 / (ws + wp)
    ws, wp = ws * inverse, wp * inverse
    for j in range(blocks):
        rows = slice(j * req_dev, (j + 1) * req_dev)
        own = jnp.broadcast_to(owner[:, j : j + 1], (req_dev, hd))
        part = f32(o_ref[0, rows, :])
        for p in range(1, n_prefix):
            part = jnp.where(own == p, f32(o_ref[p, rows, :]), part)
        mine = scr[pl.ds(j * stride, req_dev), :]
        out_ref[rows, :] = bf16(mine * ws[:, j : j + 1] + part * wp[:, j : j + 1])


def combine(got, prefix_o, prefix_lse, req_dev):
    n_rows, hd = prefix_o.shape[1:]
    vmem = pl.BlockSpec(memory_space=pltpu.VMEM)
    return pl.pallas_call(
        functools.partial(combine_kernel, req_dev=req_dev),
        name="combine",
        out_shape=jax.ShapeDtypeStruct((n_rows, hd), jnp.bfloat16),
        in_specs=[vmem] * 3,
        out_specs=vmem,
        scratch_shapes=[pltpu.VMEM(got.shape, jnp.float32)],
        compiler_params=pltpu.CompilerParams(vmem_limit_bytes=16 << 20),
        cost_estimate=pl.CostEstimate(flops=10 * n_rows * hd, bytes_accessed=12 * n_rows * hd, transcendentals=0),
    )(got, prefix_o, prefix_lse)


def exchange(x):
    return lax.all_to_all(x, BLK, split_axis=0, concat_axis=0, tiled=True)


def body(queries, prefix_kv, page_counts, request_prefix, suffix_kv, suffix_len):
    blocks = lax.axis_size(BLK)
    req_dev = suffix_kv.shape[0]
    kv_heads = suffix_kv.shape[2]
    hd = suffix_kv.shape[3] // 2
    page = prefix_kv.shape[1]
    share = blocks // kv_heads
    tok = page // share

    mine = prefix_kv[0].reshape(share, tok, kv_heads, 2, hd).transpose(2, 0, 3, 1, 4)
    mine = mine.reshape(blocks, 2 * tok, hd)
    got = exchange(jnp.concatenate([queries.reshape(blocks, req_dev, hd), mine], axis=1))

    own = got[:, req_dev:, :]
    chips = lax.axis_size("chip")
    swap = [(i, CORES - 1 - i) for i in range(CORES)]
    chunks = [own]
    owner = request_prefix[:, 0].astype(jnp.float32)[None, :]
    owner_row = jnp.pad(owner, ((0, 0), (hd - req_dev, 0)))
    for k in range(1, chips):
        chunks.append(lax.ppermute(own, "chip", [(i, (i + k) % chips) for i in range(chips)]))
    chunks = chunks + [lax.ppermute(c, "core", swap) for c in chunks]
    sent = suffix_attention(got, owner_row, suffix_kv.reshape(req_dev, -1, 2 * hd), suffix_len, kv_heads)
    back = exchange(sent.reshape(blocks, (req_dev + 2) // 2, 2, hd)).reshape(sent.shape)
    prefix_o, prefix_lse = prefix_attention(queries, chunks, page_counts, req_dev)
    return combine(back, prefix_o, prefix_lse, req_dev)


def solution(mesh):
    chips = mesh.shape["blk"] // (SEGS * CORES)
    split = Mesh(
        mesh.devices.reshape(mesh.shape["groups"], SEGS, chips, CORES), ("groups", "seg", "chip", "core")
    )
    in_specs = (
        P("groups", BLK),
        P(GROUPS_BLK, None, None, None),
        P("groups"),
        P(GROUPS_BLK, None),
        P(GROUPS_BLK, None, None, None),
        P(GROUPS_BLK),
    )
    return jax.shard_map(body, mesh=split, in_specs=in_specs, out_specs=P("groups", BLK), check_vma=False)
```

profile of v0, /device:TPU:44, one launch (start us, length us, event | category | flops | bytes accessed | tf_op | source)
XLA Modules:
  0.0 253.6 jit_solution(11581489428470401764)
XLA Ops:
  0.0 1.0 copy.7
  1.0 0.0 copy-start.3
  1.0 2.0 pad_maximum_fusion
  3.0 34.2 %all-to-all-start = ((bf16[64,48,128]{2,1,0:T(8,128)(2,1)}), bf16[64,48,128]{2,1,0:T(8,128)(2,1)S(1)}, u32[]{:S(2)}, u32[]{:S(2)}) async-start(bf16[64,48,128]{2,1,0:T(8,128)(2,1)} %pad_maximum_fusion), calls=%async_computation | async-start | bytes 1572864 | tf_op jit(solution)/shard_map/all_to_all | solution.py:294
  37.3 0.0 copy-done.3
  37.3 0.6 pad.4.owner_ref
  37.9 86.1 %all-to-all-done.got_ref = bf16[64,48,128]{2,1,0:T(8,128)(2,1)S(1)} async-done(((bf16[64,48,128]{2,1,0:T(8,128)(2,1)}), bf16[64,48,128]{2,1,0:T(8,128)(2,1)S(1)}, u32[]{:S(2)}, u32[]{:S(2)}) %all-to-all-start) | async-done | bytes 786464 | tf_op jit(solution)/shard_map/all_to_all | solution.py:294
  124.0 0.0 copy-start.2
  124.0 0.9 copy-done.2
  124.9 6.9 %suffix.1 = bf16[2176,128]{1,0:T(8,128)(2,1)} custom-call(s32[32]{0:T(128)} %len_ref.1, bf16[64,48,128]{2,1,0:T(8,128)(2,1)} %copy-done.2, f32[1,128]{1,0:T(1,128)} %pad.4.owner_ref, bf16[32,512,256]{2,1,0:T(8,128)(2,1)} %bitcast.12), custom_call_target="tpu_custom_call" | custom-call | flops 536870912 | bytes 8388608 | tf_op jit(solution)/shard_map/suffix/pallas_call | solution.py:120
  131.8 0.0 copy-start
  131.8 0.0 copy-start.1
  131.8 6.6 %all-to-all-start.1 = ((bf16[64,17,2,128]{3,2,1,0:T(2,128)(2,1)}), bf16[64,17,2,128]{3,2,1,0:T(2,128)(2,1)S(1)}, u32[]{:S(2)}, u32[]{:S(2)}) async-start(bf16[64,17,2,128]{3,2,1,0:T(2,128)(2,1)} %bitcast.13), calls=%async_computation.1 | async-start | bytes 1114112 | tf_op jit(solution)/shard_map/all_to_all | solution.py:294
  138.5 1.0 slice.4.refs_0_
  139.4 2.4 collective-permute-start.2
  141.8 0.0 collective-permute-start.1
  141.8 1.1 collective-permute-start
  142.9 0.0 collective-permute-start.3
  142.9 49.1 %collective-permute-done.2.refs_3_ = bf16[64,16,128]{2,1,0:T(8,128)(2,1)S(1)} collective-permute-done((bf16[64,16,128]{2,1,0:T(8,128)(2,1)S(1)}, bf16[64,16,128]{2,1,0:T(8,128)(2,1)S(1)}, u32[]{:S(2)}, u32[]{:S(2)}) %collective-permute-start.2) | collective-permute-done | bytes 262176 | tf_op jit(solution)/shard_map/ppermute | solution.py:317
  192.0 0.0 collective-permute-start.6
  192.1 18.1 %collective-permute-done.1.refs_2_ = bf16[64,16,128]{2,1,0:T(8,128)(2,1)S(1)} collective-permute-done((bf16[64,16,128]{2,1,0:T(8,128)(2,1)S(1)}, bf16[64,16,128]{2,1,0:T(8,128)(2,1)S(1)}, u32[]{:S(2)}, u32[]{:S(2)}) %collective-permute-start.1) | collective-permute-done | bytes 262176 | tf_op jit(solution)/shard_map/ppermute | solution.py:317
  210.2 0.0 collective-permute-start.5
  210.2 0.0 collective-permute-done.refs_1_
  210.2 0.5 collective-permute-start.4
  210.7 0.0 collective-permute-done.3.refs_4_
  210.7 0.0 collective-permute-done.6.refs_7_
  210.7 1.0 collective-permute-done.5.refs_6_
  211.7 0.4 collective-permute-done.4.refs_5_
  212.1 0.0 copy-done
  212.1 0.0 copy-done.1
  212.1 39.5 %prefix.1 = (bf16[4,2048,128]{2,1,0:T(8,128)(2,1)S(1)}, f32[4,32,128]{2,1,0:T(8,128)S(1)}) custom-call(s32[4]{0:T(128)S(1)} %copy-done.1, bf16[2048,128]{1,0:T(8,128)(2,1)S(1)} %copy-done, bf16[64,16,128]{2,1,0:T(8,128)(2,1)S(1)} %slice.4.refs_0_, bf16[64,16,128]{2,1,0:T(8,128)(2,1)S(1)} %collective-permute-done.refs_1_, ...), custom_call_target="tpu_custom_call" | custom-call | flops 4294967296 | bytes 1048576 | tf_op jit(solution)/shard_map/prefix/pallas_call | solution.py:221
  251.5 0.0 all-to-all-done.1
  251.5 2.1 combine.1
  (1 shorter events, 0.0 us)
Async XLA Ops:
  1.0 36.3 %copy-start.3 = (s32[32,1]{0,1:T(1,128)S(1)}, s32[32,1]{0,1:T(1,128)}, u32[]{:S(2)}) copy-start(s32[32,1]{0,1:T(1,128)} %param.9) | copy-start | bytes 388
  3.0 120.9 %all-to-all-start = ((bf16[64,48,128]{2,1,0:T(8,128)(2,1)}), bf16[64,48,128]{2,1,0:T(8,128)(2,1)S(1)}, u32[]{:S(2)}, u32[]{:S(2)}) async-start(bf16[64,48,128]{2,1,0:T(8,128)(2,1)} %pad_maximum_fusion), calls=%async_computation | async-start | bytes 1572864 | tf_op jit(solution)/shard_map/all_to_all | solution.py:294
  124.0 0.9 copy-start.2
  131.8 80.3 %copy-start = (bf16[2048,128]{1,0:T(8,128)(2,1)S(1)}, bf16[2048,128]{1,0:T(8,128)(2,1)}, u32[]{:S(2)}) copy-start(bf16[2048,128]{1,0:T(8,128)(2,1)} %q_ref.1) | copy-start | bytes 1572868
  131.8 80.3 %copy-start.1 = (s32[4]{0:T(128)S(1)}, s32[4]{0:T(128)}, u32[]{:S(2)}) copy-start(s32[4]{0:T(128)} %count_ref.1) | copy-start | bytes 52
  131.8 119.7 %all-to-all-start.1 = ((bf16[64,17,2,128]{3,2,1,0:T(2,128)(2,1)}), bf16[64,17,2,128]{3,2,1,0:T(2,128)(2,1)S(1)}, u32[]{:S(2)}, u32[]{:S(2)}) async-start(bf16[64,17,2,128]{3,2,1,0:T(2,128)(2,1)} %bitcast.13), calls=%async_computation.1 | async-start | bytes 1114112 | tf_op jit(solution)/shard_map/all_to_all | solution.py:294
  139.4 52.6 %collective-permute-start.2 = (bf16[64,16,128]{2,1,0:T(8,128)(2,1)S(1)}, bf16[64,16,128]{2,1,0:T(8,128)(2,1)S(1)}, u32[]{:S(2)}, u32[]{:S(2)}) collective-permute-start(bf16[64,16,128]{2,1,0:T(8,128)(2,1)S(1)} %slice.4.refs_0_), channel_id=1, source_target_pairs={{0,6},{2,0},{4,2},{6,4},{1,7},{3,1},{5,3},{7,5},{8,14},{10,8},{12,... | collective-permute-start | bytes 786440 | tf_op jit(solution)/shard_map/ppermute | solution.py:317
  141.8 68.3 %collective-permute-start.1 = (bf16[64,16,128]{2,1,0:T(8,128)(2,1)S(1)}, bf16[64,16,128]{2,1,0:T(8,128)(2,1)S(1)}, u32[]{:S(2)}, u32[]{:S(2)}) collective-permute-start(bf16[64,16,128]{2,1,0:T(8,128)(2,1)S(1)} %slice.4.refs_0_), channel_id=1, source_target_pairs={{0,4},{2,6},{4,0},{6,2},{1,5},{3,7},{5,1},{7,3},{8,12},{10,14},{12... | collective-permute-start | bytes 786440 | tf_op jit(solution)/shard_map/ppermute | solution.py:317
  141.8 68.3 %collective-permute-start = (bf16[64,16,128]{2,1,0:T(8,128)(2,1)S(1)}, bf16[64,16,128]{2,1,0:T(8,128)(2,1)S(1)}, u32[]{:S(2)}, u32[]{:S(2)}) collective-permute-start(bf16[64,16,128]{2,1,0:T(8,128)(2,1)S(1)} %slice.4.refs_0_), channel_id=1, source_target_pairs={{0,2},{2,4},{4,6},{6,0},{1,3},{3,5},{5,7},{7,1},{8,10},{10,12},{12... | collective-permute-start | bytes 786440 | tf_op jit(solution)/shard_map/ppermute | solution.py:317
  142.9 67.8 %collective-permute-start.3 = (bf16[64,16,128]{2,1,0:T(8,128)(2,1)S(1)}, bf16[64,16,128]{2,1,0:T(8,128)(2,1)S(1)}, u32[]{:S(2)}, u32[]{:S(2)}) collective-permute-start(bf16[64,16,128]{2,1,0:T(8,128)(2,1)S(1)} %slice.4.refs_0_), channel_id=1, source_target_pairs={{0,1},{1,0},{2,3},{3,2},{4,5},{5,4},{6,7},{7,6},{8,9},{9,8},{10,11... | collective-permute-start | bytes 786440 | tf_op jit(solution)/shard_map/ppermute | solution.py:318
  192.0 18.6 %collective-permute-start.6 = (bf16[64,16,128]{2,1,0:T(8,128)(2,1)S(1)}, bf16[64,16,128]{2,1,0:T(8,128)(2,1)S(1)}, u32[]{:S(2)}, u32[]{:S(2)}) collective-permute-start(bf16[64,16,128]{2,1,0:T(8,128)(2,1)S(1)} %collective-permute-done.2.refs_3_), channel_id=1, source_target_pairs={{0,1},{1,0},{2,3},{3,2},{4,5},{5,4},{6,7},{7,6},{8,9},{9,8},{10,11... | collective-permute-start | bytes 786440 | tf_op jit(solution)/shard_map/ppermute | solution.py:318
  210.2 1.5 collective-permute-start.5
  210.2 1.9 collective-permute-start.4
where the time goes:
time: 255 us; the launch traced here: 254 us
  waiting for transfers between devices  155 us (61%)
  Pallas kernels  48.4 us (19%)
  starting transfers between devices  44.9 us (18%)
  local copies, waits for them, and re-layouts  3.51 us (1%)
    all_to_all x2, waiting for transfers between devices, exchange(): return lax.all_to_all(x, BLK, split_axis=0, concat_axis=0, tiled=True)  86.1 us
    ppermute x3, waiting for transfers between devices, body(): lax.ppermute(own, 'chip', [(i, (i + k) % chips) for i in range(chips)])  67.2 us
    all_to_all x2, starting transfers between devices, exchange(): return lax.all_to_all(x, BLK, split_axis=0, concat_axis=0, tiled=True)  40.9 us
    pallas_call x1, Pallas kernels, prefix_attention(): pl.pallas_call(kernel, name='prefix', out_shape=(jax.ShapeDtypeStruct((n_...  39.5 us
    pallas_call x1, Pallas kernels, suffix_attention(): pl.pallas_call(kernel, name='suffix', out_shape=jax.ShapeDtypeStruct((row...  6.92 us
  transfers between devices with their start and end apart: 9, of which 5 were waited for; matrix products, arithmetic and copies ran while one was open for 1% of the time, Pallas kernels for 16%

commit v1 on v0

--- a/solution.py
+++ b/solution.py
@@ -19,8 +19,9 @@
 NEG = -1e30
 
 REQ_STEP = 8
-TOK_BLOCK = 512
-ROW_BLOCK = 512
+EARLY_BLOCK = 256
+LATE_BLOCK = 512
+ROW_BLOCK = 2048
 
 NT = (((1,), (1,)), ((), ()))
 
@@ -142,16 +143,21 @@
     )(suffix_len, got, owner_row, cache)
 
 
-def prefix_kernel(count_ref, q_ref, *refs, req_dev, n_chunks):
-    chunks = refs[:n_chunks]
-    o_ref, lse_ref, k_scr, v_scr, top_scr, sum_scr, acc_scr = refs[n_chunks:]
+def prefix_kernel(count_ref, q_ref, *refs, req_dev, n_chunks, block, last):
+    chunks, refs = refs[:n_chunks], refs[n_chunks:]
+    if last:
+        prev_o_ref, prev_lse_ref = refs[:2]
+        refs = refs[2:]
+    o_ref, lse_ref, k_scr, v_scr, s_scr, top_scr, sum_scr, acc_scr = refs
     n_prefix = o_ref.shape[0]
-    n_rows, hd = q_ref.shape
+    hd = q_ref.shape[1]
     pages, both = chunks[0].shape[:2]
     tok = both // 2
     page = tok * n_chunks
     scale = hd**-0.5 * LOG2E
     tail = k_scr.shape[0] - pages * page
+    row_block = top_scr.shape[0]
+    groups = row_block // req_dev
 
     @pl.loop(0, pages)
     def _(p):
@@ -164,81 +170,98 @@
     k_scr[pl.ds(pages * page, tail), :] = jnp.zeros((tail, hd), jnp.bfloat16)
     v_scr[pl.ds(pages * page, tail), :] = jnp.zeros((tail, hd), jnp.bfloat16)
 
-    col = lax.broadcasted_iota(jnp.int32, (1, TOK_BLOCK), 1)
-    lane = lax.broadcasted_iota(jnp.int32, (req_dev, lse_ref.shape[2]), 1)
-    for p in range(n_prefix):
-        lse_ref[p] = jnp.zeros(lse_ref.shape[1:], jnp.float32)
-    first = 0
-    for p in range(n_prefix):
+    col = lax.broadcasted_iota(jnp.int32, (1, block), 1)
+    tiles = [slice(k, k + hd) for k in range(0, block, hd)]
+    if last:
+        lane = lax.broadcasted_iota(jnp.int32, (req_dev, lse_ref.shape[2]), 1)
+        lse_ref[...] = jnp.zeros_like(lse_ref)
+
+    def one_prefix(p, first):
         start = first * page
         live = count_ref[p] * page
-
-        @pl.loop(0, n_rows // ROW_BLOCK)
+        steps = (live + block - 1) // block
+
+        @pl.loop(0, q_ref.shape[0] // row_block)
         def _(rb):
-            rows = pl.ds(pl.multiple_of(rb * ROW_BLOCK, ROW_BLOCK), ROW_BLOCK)
+            rows = pl.ds(pl.multiple_of(rb * row_block, row_block), row_block)
             top_scr[...] = jnp.full_like(top_scr, NEG)
+
+            @pl.loop(0, steps)
+            def _(b):
+                at = pl.ds(pl.multiple_of(start + b * block, page), block)
+                s = lax.dot_general(q_ref[rows, :], k_scr[at, :], NT, preferred_element_type=jnp.float32)
+                s = s + jnp.where(col < live - b * block, 0.0, NEG)
+                s_scr[b] = s
+                top_scr[...] = jnp.maximum(top_scr[...], functools.reduce(jnp.maximum, [s[:, k] for k in tiles]))
+
+            top = jnp.max(top_scr[...], axis=1, keepdims=True) * scale
+            top = jnp.broadcast_to(top, top_scr.shape)
+            if last:
+                prev = prev_lse_ref[p, rows, :] * LOG2E
+                top = jnp.maximum(top, prev)
+                acc_scr[...] = f32(prev_o_ref[p, rows, :]) * jnp.exp2(prev - top)
+            else:
+                acc_scr[...] = jnp.zeros_like(acc_scr)
+            top_scr[...] = top
             sum_scr[...] = jnp.zeros_like(sum_scr)
-            acc_scr[...] = jnp.zeros_like(acc_scr)
-
-            @pl.loop(0, (live + TOK_BLOCK - 1) // TOK_BLOCK)
+
+            @pl.loop(0, steps)
             def _(b):
-                at = pl.ds(pl.multiple_of(start + b * TOK_BLOCK, page), TOK_BLOCK)
-                s = lax.dot_general(q_ref[rows, :], k_scr[at, :], NT, preferred_element_type=jnp.float32)
-                past = jnp.where(col < live - b * TOK_BLOCK, 0.0, NEG)
-                s = s * scale + past
-                old = top_scr[...]
-                new = jnp.maximum(old, jnp.max(s, axis=1, keepdims=True))
-                alpha = jnp.exp2(old - new)
-                w = jnp.exp2(s - new[:, 0:1])
-                part = w[:, 0:hd]
-                for k in range(hd, TOK_BLOCK, hd):
-                    part = part + w[:, k : k + hd]
-                top_scr[...] = new
-                sum_scr[...] = sum_scr[...] * alpha + part
-                acc_scr[...] = acc_scr[...] * alpha + jnp.dot(
-                    bf16(w), v_scr[at, :], preferred_element_type=jnp.float32
-                )
-
-            total = jnp.sum(sum_scr[...], axis=1, keepdims=True)
+                at = pl.ds(pl.multiple_of(start + b * block, page), block)
+                parts = [jnp.exp2(s_scr[b, :, k] * scale - top_scr[...]) for k in tiles]
+                sum_scr[...] += functools.reduce(jnp.add, parts)
+                w = jnp.concatenate([bf16(x) for x in parts], axis=1)
+                acc_scr[...] += jnp.dot(w, v_scr[at, :], preferred_element_type=jnp.float32)
+
+            total = jnp.broadcast_to(jnp.sum(sum_scr[...], axis=1, keepdims=True), sum_scr.shape)
+            if last:
+                total = total + jnp.exp2(prev_lse_ref[p, rows, :] * LOG2E - top_scr[...])
             o_ref[p, rows, :] = bf16(acc_scr[...] / total)
-            value = top_scr[...][:, 0:1] * LN2 + jnp.log(total)
-            lse = lse_ref[p]
-            for k in range(ROW_BLOCK // req_dev):
-                piece = value[k * req_dev : (k + 1) * req_dev, :]
-                lse = jnp.where(lane == rb * (ROW_BLOCK // req_dev) + k, piece, lse)
-            lse_ref[p] = lse
-
-        first = first + count_ref[p]
-
-
-def prefix_attention(queries, chunks, page_counts, req_dev):
+            value = top_scr[...] * LN2 + jnp.log(total)
+            if last:
+                lse = lse_ref[p]
+                for k in range(groups):
+                    lse = jnp.where(lane == rb * groups + k, value[k * req_dev : (k + 1) * req_dev, :], lse)
+                lse_ref[p] = lse
+            else:
+                lse_ref[p, rows, :] = value
+
+        return first + count_ref[p]
+
+    lax.fori_loop(0, n_prefix, one_prefix, 0)
+
+
+def prefix_attention(queries, chunks, page_counts, req_dev, block, earlier=()):
     n_rows, hd = queries.shape
     n_prefix = page_counts.shape[0]
     pages, both, _ = chunks[0].shape
     tokens = pages * (both // 2) * len(chunks)
+    last = len(earlier) > 0
+    row_block = min(ROW_BLOCK, n_rows)
     vmem = pl.BlockSpec(memory_space=pltpu.VMEM)
-    kernel = functools.partial(prefix_kernel, req_dev=req_dev, n_chunks=len(chunks))
+    kernel = functools.partial(prefix_kernel, req_dev=req_dev, n_chunks=len(chunks), block=block, last=last)
     return pl.pallas_call(
         kernel,
-        name="prefix",
+        name="prefix" if last else "prefix_early",
         out_shape=(
             jax.ShapeDtypeStruct((n_prefix, n_rows, hd), jnp.bfloat16),
-            jax.ShapeDtypeStruct((n_prefix, req_dev, hd), jnp.float32),
+            jax.ShapeDtypeStruct((n_prefix, req_dev if last else n_rows, hd), jnp.float32),
         ),
-        in_specs=[pl.BlockSpec(memory_space=pltpu.SMEM)] + [vmem] * (1 + len(chunks)),
+        in_specs=[pl.BlockSpec(memory_space=pltpu.SMEM)] + [vmem] * (1 + len(chunks) + len(earlier)),
         out_specs=(vmem, vmem),
         scratch_shapes=[
-            pltpu.VMEM((tokens + TOK_BLOCK, hd), jnp.bfloat16),
-            pltpu.VMEM((tokens + TOK_BLOCK, hd), jnp.bfloat16),
-            pltpu.VMEM((ROW_BLOCK, hd), jnp.float32),
-            pltpu.VMEM((ROW_BLOCK, hd), jnp.float32),
-            pltpu.VMEM((ROW_BLOCK, hd), jnp.float32),
+            pltpu.VMEM((tokens + block, hd), jnp.bfloat16),
+            pltpu.VMEM((tokens + block, hd), jnp.bfloat16),
+            pltpu.VMEM((pl.cdiv(tokens // 2, block), row_block, block), jnp.float32),
+            pltpu.VMEM((row_block, hd), jnp.float32),
+            pltpu.VMEM((row_block, hd), jnp.float32),
+            pltpu.VMEM((row_block, hd), jnp.float32),
         ],
-        compiler_params=pltpu.CompilerParams(vmem_limit_bytes=24 << 20),
+        compiler_params=pltpu.CompilerParams(vmem_limit_bytes=(40 << 20) if last else (24 << 20)),
         cost_estimate=pl.CostEstimate(
             flops=4 * n_rows * tokens * hd, bytes_accessed=4 * n_rows * hd, transcendentals=n_rows * tokens
         ),
-    )(page_counts, queries, *chunks)
+    )(page_counts, queries, *chunks, *earlier)
 
 
 def combine_kernel(got_ref, o_ref, lse_ref, out_ref, scr, *, req_dev):
@@ -310,15 +333,18 @@
     own = got[:, req_dev:, :]
     chips = lax.axis_size("chip")
     swap = [(i, CORES - 1 - i) for i in range(CORES)]
-    chunks = [own]
     owner = request_prefix[:, 0].astype(jnp.float32)[None, :]
     owner_row = jnp.pad(owner, ((0, 0), (hd - req_dev, 0)))
-    for k in range(1, chips):
-        chunks.append(lax.ppermute(own, "chip", [(i, (i + k) % chips) for i in range(chips)]))
-    chunks = chunks + [lax.ppermute(c, "core", swap) for c in chunks]
-    sent = suffix_attention(got, owner_row, suffix_kv.reshape(req_dev, -1, 2 * hd), suffix_len, kv_heads)
+    turned = [
+        lax.ppermute(own, "chip", [(i, (i + k) % chips) for i in range(chips)]) for k in range(1, chips)
+    ]
+    cache = suffix_kv.reshape(req_dev, -1, 2 * hd)
+    sent = suffix_attention(got, owner_row, cache, suffix_len, kv_heads)
     back = exchange(sent.reshape(blocks, (req_dev + 2) // 2, 2, hd)).reshape(sent.shape)
-    prefix_o, prefix_lse = prefix_attention(queries, chunks, page_counts, req_dev)
+    chunks = [own, lax.ppermute(own, "core", swap)]
+    earlier = prefix_attention(queries, chunks, page_counts, req_dev, EARLY_BLOCK)
+    chunks = turned + [lax.ppermute(c, "core", swap) for c in turned]
+    prefix_o, prefix_lse = prefix_attention(queries, chunks, page_counts, req_dev, LATE_BLOCK, earlier)
     return combine(back, prefix_o, prefix_lse, req_dev)
 
 

time: 255 us -> 241 us (0.945)
  Pallas kernels: 48.4 us -> 35.6 us
    pallas_call x1 -> x2, Pallas kernels: 39.5 us -> 26.6 us  [prefix_attention(): pl.pallas_call(kernel, name='prefix' if last else 'prefix_early', out_sha...]
  transfers between devices with their start and end apart: 9 -> 9, of which waited for: 5 -> 3; matrix products, arithmetic and copies ran while one was open for 1% -> 1% of each run, Pallas kernels for 16% -> 11%
where the time goes in v1:
time: 241 us; the launch traced here: 239 us
  waiting for transfers between devices  153 us (63%)
  starting transfers between devices  44.7 us (19%)
  Pallas kernels  35.6 us (15%)
  local copies, waits for them, and re-layouts  3.51 us (1%)
    all_to_all x2, waiting for transfers between devices, exchange(): return lax.all_to_all(x, BLK, split_axis=0, concat_axis=0, tiled=True)  86.1 us
    ppermute x3, waiting for transfers between devices, body(): lax.ppermute(own, 'chip', [(i, (i + k) % chips) for i in range(chips)])  67.2 us
    all_to_all x2, starting transfers between devices, exchange(): return lax.all_to_all(x, BLK, split_axis=0, concat_axis=0, tiled=True)  40.7 us
    pallas_call x2, Pallas kernels, prefix_attention(): pl.pallas_call(kernel, name='prefix' if last else 'prefix_early', out_sha...  26.6 us
    pallas_call x1, Pallas kernels, suffix_attention(): pl.pallas_call(kernel, name='suffix', out_shape=jax.ShapeDtypeStruct((row...  6.97 us
  transfers between devices with their start and end apart: 9, of which 3 were waited for; matrix products, arithmetic and copies ran while one was open for 1% of the time, Pallas kernels for 11%

profile of v1, /device:TPU:44, one launch (start us, length us, event | category | flops | bytes accessed | tf_op | source)
XLA Modules:
  0.0 239.3 jit_solution(8570241647269279961)
XLA Ops:
  0.0 0.0 copy-start.3
  0.0 1.0 copy.7
  1.0 2.0 pad_maximum_fusion
  3.0 34.2 %all-to-all-start = ((bf16[64,48,128]{2,1,0:T(8,128)(2,1)}), bf16[64,48,128]{2,1,0:T(8,128)(2,1)S(1)}, u32[]{:S(2)}, u32[]{:S(2)}) async-start(bf16[64,48,128]{2,1,0:T(8,128)(2,1)} %pad_maximum_fusion), calls=%async_computation | async-start | bytes 1572864 | tf_op jit(solution)/shard_map/all_to_all | solution.py:317
  37.3 0.0 copy-done.3
  37.3 0.6 pad.4.owner_ref
  37.9 86.1 %all-to-all-done.got_ref = bf16[64,48,128]{2,1,0:T(8,128)(2,1)S(1)} async-done(((bf16[64,48,128]{2,1,0:T(8,128)(2,1)}), bf16[64,48,128]{2,1,0:T(8,128)(2,1)S(1)}, u32[]{:S(2)}, u32[]{:S(2)}) %all-to-all-start) | async-done | bytes 786464 | tf_op jit(solution)/shard_map/all_to_all | solution.py:317
  124.0 0.0 copy-start.2
  124.0 0.9 copy-done.2
  124.9 0.0 copy-start
  124.9 0.0 copy-start.1
  124.9 7.0 %suffix.1 = bf16[2176,128]{1,0:T(8,128)(2,1)} custom-call(s32[32]{0:T(128)} %len_ref.1, bf16[64,48,128]{2,1,0:T(8,128)(2,1)} %copy-done.2, f32[1,128]{1,0:T(1,128)} %pad.4.owner_ref, bf16[32,512,256]{2,1,0:T(8,128)(2,1)} %bitcast.12), custom_call_target="tpu_custom_call" | custom-call | flops 536870912 | bytes 8388608 | tf_op jit(solution)/shard_map/suffix/pallas_call | solution.py:121
  131.8 6.5 %all-to-all-start.1 = ((bf16[64,17,2,128]{3,2,1,0:T(2,128)(2,1)}), bf16[64,17,2,128]{3,2,1,0:T(2,128)(2,1)S(1)}, u32[]{:S(2)}, u32[]{:S(2)}) async-start(bf16[64,17,2,128]{3,2,1,0:T(2,128)(2,1)} %bitcast.13), calls=%async_computation.1 | async-start | bytes 1114112 | tf_op jit(solution)/shard_map/all_to_all | solution.py:317
  138.4 1.0 slice.4.refs_0_
  139.3 2.4 collective-permute-start.2
  141.7 0.0 collective-permute-start.1
  141.7 1.1 collective-permute-start
  142.8 0.0 collective-permute-start.6
  142.8 49.1 %collective-permute-done.2.refs_2_ = bf16[64,16,128]{2,1,0:T(8,128)(2,1)S(1)} collective-permute-done((bf16[64,16,128]{2,1,0:T(8,128)(2,1)S(1)}, bf16[64,16,128]{2,1,0:T(8,128)(2,1)S(1)}, u32[]{:S(2)}, u32[]{:S(2)}) %collective-permute-start.2) | collective-permute-done | bytes 262176 | tf_op jit(solution)/shard_map/ppermute | solution.py:339
  191.9 0.0 collective-permute-start.5
  192.0 18.1 %collective-permute-done.1.refs_1_ = bf16[64,16,128]{2,1,0:T(8,128)(2,1)S(1)} collective-permute-done((bf16[64,16,128]{2,1,0:T(8,128)(2,1)S(1)}, bf16[64,16,128]{2,1,0:T(8,128)(2,1)S(1)}, u32[]{:S(2)}, u32[]{:S(2)}) %collective-permute-start.1) | collective-permute-done | bytes 262176 | tf_op jit(solution)/shard_map/ppermute | solution.py:339
  210.1 0.0 collective-permute-start.4
  210.1 0.0 collective-permute-done.refs_0_
  210.1 0.5 collective-permute-start.3
  210.6 0.0 collective-permute-done.6.refs_1_
  210.6 0.0 copy-done
  210.6 0.0 copy-done.1
  210.6 9.1 %prefix_early.1 = (bf16[4,2048,128]{2,1,0:T(8,128)(2,1)S(1)}, f32[4,2048,128]{2,1,0:T(8,128)S(1)}) custom-call(s32[4]{0:T(128)S(1)} %copy-done.1, bf16[2048,128]{1,0:T(8,128)(2,1)S(1)} %copy-done, bf16[64,16,128]{2,1,0:T(8,128)(2,1)S(1)} %slice.4.refs_0_, bf16[64,16,128]{2,1,0:T(8,128)(2,1)S(1)} %collective-permute-done.6.refs_1_), custom_call_target="tpu_custom_call" | custom-call | flops 1073741824 | bytes 1048576 | tf_op jit(solution)/shard_map/prefix_early/pallas_call | solution.py:243
  219.7 0.0 collective-permute-done.5.refs_5_
  219.7 0.0 collective-permute-done.4.refs_4_
  219.7 0.0 collective-permute-done.3.refs_3_
  219.7 17.5 %prefix.1 = (bf16[4,2048,128]{2,1,0:T(8,128)(2,1)S(1)}, f32[4,32,128]{2,1,0:T(8,128)S(1)}) custom-call(s32[4]{0:T(128)S(1)} %copy-done.1, bf16[2048,128]{1,0:T(8,128)(2,1)S(1)} %copy-done, bf16[64,16,128]{2,1,0:T(8,128)(2,1)S(1)} %collective-permute-done.refs_0_, bf16[64,16,128]{2,1,0:T(8,128)(2,1)S(1)} %collective-permute-done.1.refs_1_, ...), custom_call_target="tpu_custom_call" | custom-call | flops 3221225472 | bytes 1048576 | tf_op jit(solution)/shard_map/prefix/pallas_call | solution.py:243
  237.3 0.0 all-to-all-done.1
  237.3 2.1 combine.1
  (1 shorter events, 0.0 us)
Async XLA Ops:
  0.0 37.3 %copy-start.3 = (s32[32,1]{0,1:T(1,128)S(1)}, s32[32,1]{0,1:T(1,128)}, u32[]{:S(2)}) copy-start(s32[32,1]{0,1:T(1,128)} %param.9) | copy-start | bytes 388
  3.0 120.9 %all-to-all-start = ((bf16[64,48,128]{2,1,0:T(8,128)(2,1)}), bf16[64,48,128]{2,1,0:T(8,128)(2,1)S(1)}, u32[]{:S(2)}, u32[]{:S(2)}) async-start(bf16[64,48,128]{2,1,0:T(8,128)(2,1)} %pad_maximum_fusion), calls=%async_computation | async-start | bytes 1572864 | tf_op jit(solution)/shard_map/all_to_all | solution.py:317
  124.0 0.9 copy-start.2
  124.9 85.7 %copy-start = (bf16[2048,128]{1,0:T(8,128)(2,1)S(1)}, bf16[2048,128]{1,0:T(8,128)(2,1)}, u32[]{:S(2)}) copy-start(bf16[2048,128]{1,0:T(8,128)(2,1)} %q_ref.3) | copy-start | bytes 1572868
  124.9 85.7 %copy-start.1 = (s32[4]{0:T(128)S(1)}, s32[4]{0:T(128)}, u32[]{:S(2)}) copy-start(s32[4]{0:T(128)} %count_ref.3) | copy-start | bytes 52
  131.8 105.4 %all-to-all-start.1 = ((bf16[64,17,2,128]{3,2,1,0:T(2,128)(2,1)}), bf16[64,17,2,128]{3,2,1,0:T(2,128)(2,1)S(1)}, u32[]{:S(2)}, u32[]{:S(2)}) async-start(bf16[64,17,2,128]{3,2,1,0:T(2,128)(2,1)} %bitcast.13), calls=%async_computation.1 | async-start | bytes 1114112 | tf_op jit(solution)/shard_map/all_to_all | solution.py:317
  139.3 52.6 %collective-permute-start.2 = (bf16[64,16,128]{2,1,0:T(8,128)(2,1)S(1)}, bf16[64,16,128]{2,1,0:T(8,128)(2,1)S(1)}, u32[]{:S(2)}, u32[]{:S(2)}) collective-permute-start(bf16[64,16,128]{2,1,0:T(8,128)(2,1)S(1)} %slice.4.refs_0_), channel_id=1, source_target_pairs={{0,6},{2,0},{4,2},{6,4},{1,7},{3,1},{5,3},{7,5},{8,14},{10,8},{12,... | collective-permute-start | bytes 786440 | tf_op jit(solution)/shard_map/ppermute | solution.py:339
  141.7 68.3 %collective-permute-start.1 = (bf16[64,16,128]{2,1,0:T(8,128)(2,1)S(1)}, bf16[64,16,128]{2,1,0:T(8,128)(2,1)S(1)}, u32[]{:S(2)}, u32[]{:S(2)}) collective-permute-start(bf16[64,16,128]{2,1,0:T(8,128)(2,1)S(1)} %slice.4.refs_0_), channel_id=1, source_target_pairs={{0,4},{2,6},{4,0},{6,2},{1,5},{3,7},{5,1},{7,3},{8,12},{10,14},{12... | collective-permute-start | bytes 786440 | tf_op jit(solution)/shard_map/ppermute | solution.py:339
  141.7 68.3 %collective-permute-start = (bf16[64,16,128]{2,1,0:T(8,128)(2,1)S(1)}, bf16[64,16,128]{2,1,0:T(8,128)(2,1)S(1)}, u32[]{:S(2)}, u32[]{:S(2)}) collective-permute-start(bf16[64,16,128]{2,1,0:T(8,128)(2,1)S(1)} %slice.4.refs_0_), channel_id=1, source_target_pairs={{0,2},{2,4},{4,6},{6,0},{1,3},{3,5},{5,7},{7,1},{8,10},{10,12},{12... | collective-permute-start | bytes 786440 | tf_op jit(solution)/shard_map/ppermute | solution.py:339
  142.8 67.8 %collective-permute-start.6 = (bf16[64,16,128]{2,1,0:T(8,128)(2,1)S(1)}, bf16[64,16,128]{2,1,0:T(8,128)(2,1)S(1)}, u32[]{:S(2)}, u32[]{:S(2)}) collective-permute-start(bf16[64,16,128]{2,1,0:T(8,128)(2,1)S(1)} %slice.4.refs_0_), channel_id=1, source_target_pairs={{0,1},{1,0},{2,3},{3,2},{4,5},{5,4},{6,7},{7,6},{8,9},{9,8},{10,11... | collective-permute-start | bytes 786440 | tf_op jit(solution)/shard_map/ppermute | solution.py:344
  191.9 27.7 %collective-permute-start.5 = (bf16[64,16,128]{2,1,0:T(8,128)(2,1)S(1)}, bf16[64,16,128]{2,1,0:T(8,128)(2,1)S(1)}, u32[]{:S(2)}, u32[]{:S(2)}) collective-permute-start(bf16[64,16,128]{2,1,0:T(8,128)(2,1)S(1)} %collective-permute-done.2.refs_2_), channel_id=1, source_target_pairs={{0,1},{1,0},{2,3},{3,2},{4,5},{5,4},{6,7},{7,6},{8,9},{9,8},{10,11... | collective-permute-start | bytes 786440 | tf_op jit(solution)/shard_map/ppermute | solution.py:346
  210.1 9.6 %collective-permute-start.4 = (bf16[64,16,128]{2,1,0:T(8,128)(2,1)S(1)}, bf16[64,16,128]{2,1,0:T(8,128)(2,1)S(1)}, u32[]{:S(2)}, u32[]{:S(2)}) collective-permute-start(bf16[64,16,128]{2,1,0:T(8,128)(2,1)S(1)} %collective-permute-done.1.refs_1_), channel_id=1, source_target_pairs={{0,1},{1,0},{2,3},{3,2},{4,5},{5,4},{6,7},{7,6},{8,9},{9,8},{10,11... | collective-permute-start | bytes 786440 | tf_op jit(solution)/shard_map/ppermute | solution.py:346
  210.1 9.6 %collective-permute-start.3 = (bf16[64,16,128]{2,1,0:T(8,128)(2,1)S(1)}, bf16[64,16,128]{2,1,0:T(8,128)(2,1)S(1)}, u32[]{:S(2)}, u32[]{:S(2)}) collective-permute-start(bf16[64,16,128]{2,1,0:T(8,128)(2,1)S(1)} %collective-permute-done.refs_0_), channel_id=1, source_target_pairs={{0,1},{1,0},{2,3},{3,2},{4,5},{5,4},{6,7},{7,6},{8,9},{9,8},{10,11... | collective-permute-start | bytes 786440 | tf_op jit(solution)/shard_map/ppermute | solution.py:346

commit v2 on v1

--- a/solution.py
+++ b/solution.py
@@ -18,7 +18,7 @@
 LN2 = 0.6931471805599453
 NEG = -1e30
 
-REQ_STEP = 8
+REQ_STEP = 4
 EARLY_BLOCK = 256
 LATE_BLOCK = 512
 ROW_BLOCK = 2048
@@ -32,6 +32,51 @@
 
 def bf16(x):
     return x.astype(jnp.bfloat16)
+
+
+def pack_kernel(q_ref, page_ref, out_ref, page_scr, key_scr, value_scr, sems):
+    req_dev = q_ref.shape[1]
+    page, kv_heads, width = page_ref.shape
+    hd = width // 2
+    share = out_ref.shape[0] // kv_heads
+    tok = page // share
+    fetch = pltpu.make_async_copy(page_ref, page_scr, sems.at[0])
+    place = pltpu.make_async_copy(q_ref, out_ref.at[:, pl.ds(0, req_dev), :], sems.at[1])
+    fetch.start()
+    place.start()
+    fetch.wait()
+    for t in range(0, page, tok):
+        at = slice(t * kv_heads, (t + tok) * kv_heads)
+        key_scr[at, :] = f32(page_scr[t : t + tok, :, 0:hd]).reshape(tok * kv_heads, hd)
+        value_scr[at, :] = f32(page_scr[t : t + tok, :, hd:width]).reshape(tok * kv_heads, hd)
+    for g in range(kv_heads):
+        for j in range(share):
+            at = pl.ds(j * tok * kv_heads + g, tok, stride=kv_heads)
+            keys, values = key_scr[at, :], value_scr[at, :]
+            out_ref[g * share + j, req_dev : req_dev + 2 * tok, :] = bf16(jnp.concatenate([keys, values], axis=0))
+    place.wait()
+
+
+def pack(queries, page_kv, blocks):
+    n_rows, hd = queries.shape
+    page, kv_heads, _ = page_kv.shape
+    req_dev = n_rows // blocks
+    rows = req_dev + 2 * page * kv_heads // blocks
+    return pl.pallas_call(
+        pack_kernel,
+        name="pack",
+        out_shape=jax.ShapeDtypeStruct((blocks, rows, hd), jnp.bfloat16),
+        in_specs=[pl.BlockSpec(memory_space=pl.ANY)] * 2,
+        out_specs=pl.BlockSpec(memory_space=pltpu.VMEM),
+        scratch_shapes=[
+            pltpu.VMEM(page_kv.shape, page_kv.dtype),
+            pltpu.VMEM((page * kv_heads, hd), jnp.float32),
+            pltpu.VMEM((page * kv_heads, hd), jnp.float32),
+            pltpu.SemaphoreType.DMA((2,)),
+        ],
+        compiler_params=pltpu.CompilerParams(vmem_limit_bytes=57 << 20),
+        cost_estimate=pl.CostEstimate(flops=0, bytes_accessed=4 * blocks * rows * hd, transcendentals=0),
+    )(queries.reshape(blocks, req_dev, hd), page_kv)
 
 
 def suffix_kernel(
@@ -322,13 +367,7 @@
     req_dev = suffix_kv.shape[0]
     kv_heads = suffix_kv.shape[2]
     hd = suffix_kv.shape[3] // 2
-    page = prefix_kv.shape[1]
-    share = blocks // kv_heads
-    tok = page // share
-
-    mine = prefix_kv[0].reshape(share, tok, kv_heads, 2, hd).transpose(2, 0, 3, 1, 4)
-    mine = mine.reshape(blocks, 2 * tok, hd)
-    got = exchange(jnp.concatenate([queries.reshape(blocks, req_dev, hd), mine], axis=1))
+    got = exchange(pack(queries, prefix_kv[0], blocks))
 
     own = got[:, req_dev:, :]
     chips = lax.axis_size("chip")

time: 241 us -> 240 us (level)
  Pallas kernels: 35.6 us -> 38.4 us
  transfers between devices with their start and end apart: 9 -> 9, of which waited for: 3 -> 3; matrix products, arithmetic and copies ran while one was open for 1% -> 1% of each run, Pallas kernels for 11% -> 12%
where the time goes in v2:
time: 240 us; the launch traced here: 239 us
  waiting for transfers between devices  153 us (64%)
  starting transfers between devices  44.7 us (19%)
  Pallas kernels  38.4 us (16%)
  local copies, waits for them, and re-layouts  2.48 us (1%)
    all_to_all x2, waiting for transfers between devices, exchange(): return lax.all_to_all(x, BLK, split_axis=0, concat_axis=0, tiled=True)  85.4 us
    ppermute x3, waiting for transfers between devices, body(): lax.ppermute(own, 'chip', [(i, (i + k) % chips) for i in range(chips)])  67.2 us
    all_to_all x2, starting transfers between devices, exchange(): return lax.all_to_all(x, BLK, split_axis=0, concat_axis=0, tiled=True)  40.7 us
    pallas_call x2, Pallas kernels, prefix_attention(): pl.pallas_call(kernel, name='prefix' if last else 'prefix_early', out_sha...  27.5 us
    pallas_call x1, Pallas kernels, suffix_attention(): pl.pallas_call(kernel, name='suffix', out_shape=jax.ShapeDtypeStruct((row...  6.8 us
  transfers between devices with their start and end apart: 9, of which 3 were waited for; matrix products, arithmetic and copies ran while one was open for 1% of the time, Pallas kernels for 12%

profile of v2, /device:TPU:44, one launch (start us, length us, event | category | flops | bytes accessed | tf_op | source)
XLA Modules:
  0.0 239.1 jit_solution(2212781604920859392)
XLA Ops:
  0.0 2.0 pack.1
  2.1 34.2 %all-to-all-start = ((bf16[64,48,128]{2,1,0:T(8,128)(2,1)}), bf16[64,48,128]{2,1,0:T(8,128)(2,1)S(1)}, u32[]{:S(2)}, u32[]{:S(2)}) async-start(bf16[64,48,128]{2,1,0:T(8,128)(2,1)} %pack.1), calls=%async_computation | async-start | bytes 1572864 | tf_op jit(solution)/shard_map/all_to_all | solution.py:362
  36.3 0.7 convert_bitcast_fusion
  37.0 0.6 pad.4.owner_ref
  37.5 85.4 %all-to-all-done.got_ref = bf16[64,48,128]{2,1,0:T(8,128)(2,1)S(1)} async-done(((bf16[64,48,128]{2,1,0:T(8,128)(2,1)}), bf16[64,48,128]{2,1,0:T(8,128)(2,1)S(1)}, u32[]{:S(2)}, u32[]{:S(2)}) %all-to-all-start) | async-done | bytes 786464 | tf_op jit(solution)/shard_map/all_to_all | solution.py:362
  123.0 0.0 copy-start.2
  123.0 0.9 copy-done.2
  123.9 0.0 copy-start
  123.9 0.0 copy-start.1
  123.9 6.8 %suffix.1 = bf16[2176,128]{1,0:T(8,128)(2,1)} custom-call(s32[32]{0:T(128)} %len_ref.1, bf16[64,48,128]{2,1,0:T(8,128)(2,1)} %copy-done.2, f32[1,128]{1,0:T(1,128)} %pad.4.owner_ref, bf16[32,512,256]{2,1,0:T(8,128)(2,1)} %bitcast.9), custom_call_target="tpu_custom_call" | custom-call | flops 536870912 | bytes 8388608 | tf_op jit(solution)/shard_map/suffix/pallas_call | solution.py:166
  130.7 6.5 %all-to-all-start.1 = ((bf16[64,17,2,128]{3,2,1,0:T(2,128)(2,1)}), bf16[64,17,2,128]{3,2,1,0:T(2,128)(2,1)S(1)}, u32[]{:S(2)}, u32[]{:S(2)}) async-start(bf16[64,17,2,128]{3,2,1,0:T(2,128)(2,1)} %bitcast.10), calls=%async_computation.1 | async-start | bytes 1114112 | tf_op jit(solution)/shard_map/all_to_all | solution.py:362
  137.2 1.0 slice.4.refs_0_
  138.2 2.4 collective-permute-start.2
  140.6 0.0 collective-permute-start.1
  140.6 1.1 collective-permute-start
  141.7 0.0 collective-permute-start.6
  141.7 49.1 %collective-permute-done.2.refs_2_ = bf16[64,16,128]{2,1,0:T(8,128)(2,1)S(1)} collective-permute-done((bf16[64,16,128]{2,1,0:T(8,128)(2,1)S(1)}, bf16[64,16,128]{2,1,0:T(8,128)(2,1)S(1)}, u32[]{:S(2)}, u32[]{:S(2)}) %collective-permute-start.2) | collective-permute-done | bytes 262176 | tf_op jit(solution)/shard_map/ppermute | solution.py:378
  190.8 0.0 collective-permute-start.5
  190.8 18.1 %collective-permute-done.1.refs_1_ = bf16[64,16,128]{2,1,0:T(8,128)(2,1)S(1)} collective-permute-done((bf16[64,16,128]{2,1,0:T(8,128)(2,1)S(1)}, bf16[64,16,128]{2,1,0:T(8,128)(2,1)S(1)}, u32[]{:S(2)}, u32[]{:S(2)}) %collective-permute-start.1) | collective-permute-done | bytes 262176 | tf_op jit(solution)/shard_map/ppermute | solution.py:378
  208.9 0.0 collective-permute-start.4
  208.9 0.0 collective-permute-done.refs_0_
  208.9 0.5 collective-permute-start.3
  209.4 0.0 collective-permute-done.6.refs_1_
  209.4 0.0 copy-done
  209.4 0.0 copy-done.1
  209.5 9.4 %prefix_early.1 = (bf16[4,2048,128]{2,1,0:T(8,128)(2,1)S(1)}, f32[4,2048,128]{2,1,0:T(8,128)S(1)}) custom-call(s32[4]{0:T(128)S(1)} %copy-done.1, bf16[2048,128]{1,0:T(8,128)(2,1)S(1)} %copy-done, bf16[64,16,128]{2,1,0:T(8,128)(2,1)S(1)} %slice.4.refs_0_, bf16[64,16,128]{2,1,0:T(8,128)(2,1)S(1)} %collective-permute-done.6.refs_1_), custom_call_target="tpu_custom_call" | custom-call | flops 1073741824 | bytes 1048576 | tf_op jit(solution)/shard_map/prefix_early/pallas_call | solution.py:288
  218.9 0.0 collective-permute-done.5.refs_5_
  218.9 0.0 collective-permute-done.4.refs_4_
  218.9 0.0 collective-permute-done.3.refs_3_
  218.9 18.1 %prefix.1 = (bf16[4,2048,128]{2,1,0:T(8,128)(2,1)S(1)}, f32[4,32,128]{2,1,0:T(8,128)S(1)}) custom-call(s32[4]{0:T(128)S(1)} %copy-done.1, bf16[2048,128]{1,0:T(8,128)(2,1)S(1)} %copy-done, bf16[64,16,128]{2,1,0:T(8,128)(2,1)S(1)} %collective-permute-done.refs_0_, bf16[64,16,128]{2,1,0:T(8,128)(2,1)S(1)} %collective-permute-done.1.refs_1_, ...), custom_call_target="tpu_custom_call" | custom-call | flops 3221225472 | bytes 1048576 | tf_op jit(solution)/shard_map/prefix/pallas_call | solution.py:288
  237.0 0.0 all-to-all-done.1
  237.0 2.1 combine.1
Async XLA Ops:
  2.1 120.9 %all-to-all-start = ((bf16[64,48,128]{2,1,0:T(8,128)(2,1)}), bf16[64,48,128]{2,1,0:T(8,128)(2,1)S(1)}, u32[]{:S(2)}, u32[]{:S(2)}) async-start(bf16[64,48,128]{2,1,0:T(8,128)(2,1)} %pack.1), calls=%async_computation | async-start | bytes 1572864 | tf_op jit(solution)/shard_map/all_to_all | solution.py:362
  123.0 0.9 copy-start.2
  123.9 85.6 %copy-start = (bf16[2048,128]{1,0:T(8,128)(2,1)S(1)}, bf16[2048,128]{1,0:T(8,128)(2,1)}, u32[]{:S(2)}) copy-start(bf16[2048,128]{1,0:T(8,128)(2,1)} %q_ref.3) | copy-start | bytes 1572868
  123.9 85.6 %copy-start.1 = (s32[4]{0:T(128)S(1)}, s32[4]{0:T(128)}, u32[]{:S(2)}) copy-start(s32[4]{0:T(128)} %count_ref.3) | copy-start | bytes 52
  130.7 106.3 %all-to-all-start.1 = ((bf16[64,17,2,128]{3,2,1,0:T(2,128)(2,1)}), bf16[64,17,2,128]{3,2,1,0:T(2,128)(2,1)S(1)}, u32[]{:S(2)}, u32[]{:S(2)}) async-start(bf16[64,17,2,128]{3,2,1,0:T(2,128)(2,1)} %bitcast.10), calls=%async_computation.1 | async-start | bytes 1114112 | tf_op jit(solution)/shard_map/all_to_all | solution.py:362
  138.2 52.6 %collective-permute-start.2 = (bf16[64,16,128]{2,1,0:T(8,128)(2,1)S(1)}, bf16[64,16,128]{2,1,0:T(8,128)(2,1)S(1)}, u32[]{:S(2)}, u32[]{:S(2)}) collective-permute-start(bf16[64,16,128]{2,1,0:T(8,128)(2,1)S(1)} %slice.4.refs_0_), channel_id=1, source_target_pairs={{0,6},{2,0},{4,2},{6,4},{1,7},{3,1},{5,3},{7,5},{8,14},{10,8},{12,... | collective-permute-start | bytes 786440 | tf_op jit(solution)/shard_map/ppermute | solution.py:378
  140.6 68.3 %collective-permute-start.1 = (bf16[64,16,128]{2,1,0:T(8,128)(2,1)S(1)}, bf16[64,16,128]{2,1,0:T(8,128)(2,1)S(1)}, u32[]{:S(2)}, u32[]{:S(2)}) collective-permute-start(bf16[64,16,128]{2,1,0:T(8,128)(2,1)S(1)} %slice.4.refs_0_), channel_id=1, source_target_pairs={{0,4},{2,6},{4,0},{6,2},{1,5},{3,7},{5,1},{7,3},{8,12},{10,14},{12... | collective-permute-start | bytes 786440 | tf_op jit(solution)/shard_map/ppermute | solution.py:378
  140.6 68.3 %collective-permute-start = (bf16[64,16,128]{2,1,0:T(8,128)(2,1)S(1)}, bf16[64,16,128]{2,1,0:T(8,128)(2,1)S(1)}, u32[]{:S(2)}, u32[]{:S(2)}) collective-permute-start(bf16[64,16,128]{2,1,0:T(8,128)(2,1)S(1)} %slice.4.refs_0_), channel_id=1, source_target_pairs={{0,2},{2,4},{4,6},{6,0},{1,3},{3,5},{5,7},{7,1},{8,10},{10,12},{12... | collective-permute-start | bytes 786440 | tf_op jit(solution)/shard_map/ppermute | solution.py:378
  141.7 67.8 %collective-permute-start.6 = (bf16[64,16,128]{2,1,0:T(8,128)(2,1)S(1)}, bf16[64,16,128]{2,1,0:T(8,128)(2,1)S(1)}, u32[]{:S(2)}, u32[]{:S(2)}) collective-permute-start(bf16[64,16,128]{2,1,0:T(8,128)(2,1)S(1)} %slice.4.refs_0_), channel_id=1, source_target_pairs={{0,1},{1,0},{2,3},{3,2},{4,5},{5,4},{6,7},{7,6},{8,9},{9,8},{10,11... | collective-permute-start | bytes 786440 | tf_op jit(solution)/shard_map/ppermute | solution.py:383
  190.8 28.0 %collective-permute-start.5 = (bf16[64,16,128]{2,1,0:T(8,128)(2,1)S(1)}, bf16[64,16,128]{2,1,0:T(8,128)(2,1)S(1)}, u32[]{:S(2)}, u32[]{:S(2)}) collective-permute-start(bf16[64,16,128]{2,1,0:T(8,128)(2,1)S(1)} %collective-permute-done.2.refs_2_), channel_id=1, source_target_pairs={{0,1},{1,0},{2,3},{3,2},{4,5},{5,4},{6,7},{7,6},{8,9},{9,8},{10,11... | collective-permute-start | bytes 786440 | tf_op jit(solution)/shard_map/ppermute | solution.py:385
  208.9 9.9 %collective-permute-start.4 = (bf16[64,16,128]{2,1,0:T(8,128)(2,1)S(1)}, bf16[64,16,128]{2,1,0:T(8,128)(2,1)S(1)}, u32[]{:S(2)}, u32[]{:S(2)}) collective-permute-start(bf16[64,16,128]{2,1,0:T(8,128)(2,1)S(1)} %collective-permute-done.1.refs_1_), channel_id=1, source_target_pairs={{0,1},{1,0},{2,3},{3,2},{4,5},{5,4},{6,7},{7,6},{8,9},{9,8},{10,11... | collective-permute-start | bytes 786440 | tf_op jit(solution)/shard_map/ppermute | solution.py:385
  208.9 9.9 %collective-permute-start.3 = (bf16[64,16,128]{2,1,0:T(8,128)(2,1)S(1)}, bf16[64,16,128]{2,1,0:T(8,128)(2,1)S(1)}, u32[]{:S(2)}, u32[]{:S(2)}) collective-permute-start(bf16[64,16,128]{2,1,0:T(8,128)(2,1)S(1)} %collective-permute-done.refs_0_), channel_id=1, source_target_pairs={{0,1},{1,0},{2,3},{3,2},{4,5},{5,4},{6,7},{7,6},{8,9},{9,8},{10,11... | collective-permute-start | bytes 786440 | tf_op jit(solution)/shard_map/ppermute | solution.py:385
